TPU v7x, 256 devices: a whole 4x4x8 slice. The times are simulated.
256 devices in a mesh: frame: 16 (over z, x_lo), row: 16 (over x_hi, y, core).
Axes of the slice: x: 4 (x_hi: 2, x_lo: 2; x = x_hi * 2 + x_lo), y: 4, z: 8, core: 2. Of those that a mesh axis runs over, the one named last changes fastest.
Arguments:
- frames: float32 [64, 512, 2048], P('frame', 'row'), may hold values from -12 to 12
Outputs:
- estimate: float32 [512, 2048], P('row')
All inputs are finite; a program needn't handle non-finite values.
Results may differ from a plain program's by a relative error of at most 0.00002.
Values sent between devices are 32-bit elements; how exact they have to be, the bound alone decides.
A program may use at most 64 MiB of HBM per device.

v0:
```python
import jax
import jax.numpy as jnp
from jax import lax
from jax.sharding import PartitionSpec as P

FRAMES = 64
ROUNDS = 3


GUIDE_EPS = 0.05
CAUCHY_SCALE = 0.5


def filled_up(lines, count):
    spare = -len(lines) % count
    return jnp.pad(lines, [(0, spare)] + [(0, 0)] * (lines.ndim - 1))


def laid_out(parts, dim):
    parts = jnp.moveaxis(parts, 0, dim)
    lengths = parts.shape
    return parts.reshape(*lengths[:dim], lengths[dim] * lengths[dim + 1], *lengths[dim + 2 :])


def copy_for_each(x, axis):
    copies = jnp.broadcast_to(x, (lax.axis_size(axis), *x.shape))
    return lax.all_to_all(copies, axis, split_axis=0, concat_axis=0, tiled=True)


def collect(x, axis, dim):
    return laid_out(copy_for_each(x, axis), dim)


def cut_along(x, dim, count):
    before, after = (x.shape[:dim], x.shape[dim + 1 :])
    return jnp.moveaxis(x.reshape(*before, count, -1, *after), dim, 0)


def summed_on_arrival(x, axis, dim):
    count = lax.axis_size(axis)
    parts = lax.all_to_all(cut_along(x, dim, count), axis, 0, 0, tiled=True)
    return jnp.sum(parts, axis=0)


def sum_by_parts(x, axes):
    lines = x.reshape(-1, x.shape[-1])
    padded = filled_up(lines, lax.axis_size(axes))
    whole = collect(summed_on_arrival(padded, axes, 0), axes, 0)
    return lax.slice_in_dim(whole, 0, len(lines)).reshape(x.shape)


def with_halo(x, sides, width):
    for axis, dim in sides:
        count, length = (lax.axis_size(axis), x.shape[dim])
        up = [(i, (i + 1) % count) for i in range(count - 1)]
        down = [(j, i) for i, j in up]
        last = lax.slice_in_dim(x, length - width, length, axis=dim)
        initial = lax.slice_in_dim(x, 0, width, axis=dim)
        before = lax.ppermute(last, axis, up)
        after = lax.ppermute(initial, axis, down)
        x = jnp.concatenate([before, x, after], axis=dim)
    return x


def side_by_side(arrays, axis, dim, along):
    ends, at = ([], 0)
    for a in arrays[:-1]:
        at += a.shape[along]
        ends.append(at)
    both = jnp.concatenate(arrays, axis=along)
    return tuple(jnp.split(summed_on_arrival(both, axis, dim), ends, axis=along))


def row_sum(field):
    length = field.shape[-2] - 8
    total = field[..., 0:length, :]
    for offset in range(1, 9):
        total = total + field[..., offset : offset + length, :]
    return total


def col_sum(field):
    width = field.shape[-1]
    padded = jnp.pad(field, [(0, 0)] * (field.ndim - 1) + [(4, 4)])
    total = padded[..., 0:width]
    for offset in range(1, 9):
        total = total + padded[..., offset : offset + width]
    return total


def window_count(first, length, limit):
    place = first + jnp.arange(length, dtype=jnp.int32)
    lower = jnp.maximum(place - 4, 0)
    upper = jnp.minimum(place + 4, limit - 1)
    return jnp.maximum(upper - lower + 1, 1).astype(jnp.float32)


def smooth(padded_rows, area):
    return col_sum(row_sum(padded_rows)) / area


def shards(frames):
    local_rows = frames.shape[1]
    width = frames.shape[2]
    height = local_rows * lax.axis_size("row")
    start = lax.axis_index("row") * local_rows
    col_counts = window_count(0, width, width)
    estimate = sum_by_parts(jnp.sum(frames, axis=0), "frame") / FRAMES
    depth = 8
    padded_frames = with_halo(frames, (("row", 1),), 8)
    stat_rows = local_rows + 2 * depth - 8
    stat_first = start - depth + 4
    stat_area = window_count(stat_first, stat_rows, height)[:, None] * col_counts[None, :]
    place = stat_first + jnp.arange(stat_rows, dtype=jnp.int32)
    inside = ((place >= 0) & (place < height)).astype(jnp.float32)[:, None]
    out_area = window_count(start, local_rows, height)[:, None] * col_counts[None, :]
    for round_index in range(ROUNDS):
        padded_guide = with_halo(estimate, (("row", 0),), 8)
        mean_guide = smooth(padded_guide, stat_area)
        variance = smooth(padded_guide * padded_guide, stat_area) - mean_guide * mean_guide
        mean_frame = smooth(padded_frames, stat_area)
        cross = smooth(padded_guide[None] * padded_frames, stat_area)
        slope = (cross - mean_guide * mean_frame) / (variance + GUIDE_EPS)
        offset_term = mean_frame - slope * mean_guide
        slope_rows = slope * inside
        offset_rows = offset_term * inside
        filtered = smooth(slope_rows, out_area) * estimate[None] + smooth(offset_rows, out_area)
        gap = (filtered - estimate[None]) / CAUCHY_SCALE
        weight = 1.0 / (1.0 + gap * gap)
        weighted = jnp.sum(weight * frames, axis=0)
        total = jnp.sum(weight, axis=0)
        shares = side_by_side((weighted, total), "frame", 1, 0)
        estimate = collect(shares[0] / shares[1], "frame", 1)
    return estimate


def solution(mesh):
    return jax.shard_map(
        shards,
        mesh=mesh,
        in_specs=(P("frame", "row", None),),
        out_specs=P("row", None),
        check_vma=False,
    )
```

profile of v0, /device:TPU:4, one launch (start us, length us, event | category | flops | bytes accessed | tf_op | source)
XLA Modules:
  0.0 230.8 jit_solution(7947396872334988032)
XLA Ops:
  0.0 1.9 fusion.48
  1.9 1.9 collective-permute-start.2
  3.8 9.4 %collective-permute-done.2 = f32[4,8,2048]{2,1,0:T(8,128)S(1)} collective-permute-done((f32[4,8,2048]{2,1,0:T(8,128)S(1)}, f32[4,8,2048]{2,1,0:T(8,128)S(1)}, u32[]{:S(2)}, u32[]{:S(2)}) %collective-permute-start.2) | collective-permute-done | bytes 262176 | tf_op jit(solution)/shard_map/ppermute | solution.py:59
  13.4 0.8 reshape.144
  14.2 9.2 %all-to-all-start = ((f32[16,2,2048]{2,1,0:T(2,128)}), f32[16,2,2048]{2,1,0:T(2,128)S(1)}, u32[]{:S(2)}, u32[]{:S(2)}) async-start(f32[16,2,2048]{2,1,0:T(2,128)} %reshape.144), calls=%async_computation | async-start | bytes 524288 | tf_op jit(solution)/shard_map/all_to_all | solution.py:41
  23.4 1.9 collective-permute-start.3
  25.4 8.8 %all-to-all-done = f32[16,2,2048]{2,1,0:T(2,128)S(1)} async-done(((f32[16,2,2048]{2,1,0:T(2,128)}), f32[16,2,2048]{2,1,0:T(2,128)S(1)}, u32[]{:S(2)}, u32[]{:S(2)}) %all-to-all-start) | async-done | bytes 262176 | tf_op jit(solution)/shard_map/all_to_all | solution.py:41
  34.2 0.8 broadcast_in_dim.8
  35.1 4.2 %all-to-all-start.1 = ((f32[16,2,2048]{2,1,0:T(2,128)}), f32[16,2,2048]{2,1,0:T(2,128)}, u32[]{:S(2)}, u32[]{:S(2)}) async-start(f32[16,2,2048]{2,1,0:T(2,128)} %broadcast_in_dim.8), calls=%async_computation.1 | async-start | bytes 524288 | tf_op jit(solution)/shard_map/all_to_all | solution.py:27
  39.4 0.7 copy-done.7
  40.1 10.2 %all-to-all-done.1 = f32[16,2,2048]{2,1,0:T(2,128)} async-done(((f32[16,2,2048]{2,1,0:T(2,128)}), f32[16,2,2048]{2,1,0:T(2,128)}, u32[]{:S(2)}, u32[]{:S(2)}) %all-to-all-start.1) | async-done | bytes 262176 | tf_op jit(solution)/shard_map/all_to_all | solution.py:27
  50.3 1.1 broadcast_multiply_fusion.8
  51.5 0.7 slice.903
  52.1 1.9 collective-permute-start
  54.0 2.9 %fusion = f32[4,40,2048]{2,1,0:T(8,128)} fusion(f32[4,48,2048]{2,1,0:T(8,128)S(1)} %constant_dynamic-update-slice_fusion.3, f32[4,32,2048]{2,1,0:T(8,128)S(1)} %copy-done, f32[4,8,2048]{2,1,0:T(8,128)S(1)} %collective-permute-done.2, f32[4,8,2048]{2,1,0:T(8,128)} %copy-done.7), kind=kLoop, calls=%fused_computation.17 | loop fusion | flops 3276800 | bytes 12058624 | tf_op jit(solution)/shard_map/add | solution.py:78
  57.0 0.2 div.74
  57.2 7.4 %collective-permute-start.1 = (f32[8,2048]{1,0:T(8,128)S(1)}, f32[8,2048]{1,0:T(8,128)S(1)}, u32[]{:S(2)}, u32[]{:S(2)}) collective-permute-start(f32[8,2048]{1,0:T(8,128)S(1)} %slice.905), channel_id=1, source_target_pairs={{1,0},{2,1},{3,2},{4,3},{5,4},{6,5},{7,6},{8,7},{9,8},{10,9},{11,1... | collective-permute-start | bytes 196616 | tf_op jit(solution)/shard_map/ppermute | solution.py:60
  64.7 1.7 collective-permute-done.1
  66.4 0.2 broadcast_multiply_fusion.2
  66.6 0.2 slice_add_fusion.109
  66.9 0.9 slice_add_fusion.23
  67.8 0.2 fusion.29
  68.1 1.4 fusion.22
  69.5 5.6 %broadcast_multiply_fusion.5 = (f32[4,40,2048]{2,1,0:T(8,128)S(1)}, f32[4,40,2048]{2,1,0:T(8,128)S(1)}, f32[4,40,2048]{2,1,0:T(8,128)S(1)}) fusion(f32[40]{0:T(128)S(1)} %and_convert_fusion, f32[40,2048]{1,0:T(8,128)S(1)} %get-tuple-element.22, f32[40,2048]{1,0:T(8,128)S(1)} %get-tuple-element.23, f32[40,2048]{1,0:T(8,128)S(1)} %get-tuple-element.34, ...), kind=kLoop, calls=%fused_computation.154 | loop fusion | flops 7208960 | bytes 7536800 | tf_op jit(solution)/shard_map/mul | solution.py:125
  75.1 0.4 subtract_multiply_fusion.2
  75.5 1.5 slice_add_fusion.63
  77.1 4.5 %multiply_reduce_fusion.2 = (f32[32,2048]{1,0:T(8,128)S(1)}, f32[32,2048]{1,0:T(8,128)S(1)}) fusion(f32[4,32,2048]{2,1,0:T(8,128)S(1)} %copy-done.1, f32[4,32,2048]{2,1,0:T(8,128)S(1)} %get-tuple-element.35, f32[32,2048]{1,0:T(8,128)S(1)} %copy-done.6, f32[32,2048]{1,0:T(8,128)S(1)} %broadcast_multiply_fusion.7, f32[4,32,2048]{2,1,0:T(8,128)S(1)} %get-tuple-element.36), kind=kLoop, calls=%fused_computation.131 | loop fusion | flops 7208960 | bytes 4194304 | tf_op jit(solution)/shard_map/reduce_sum | solution.py:130
  82.0 17.0 %all_to_all.40 = f32[16,64,128]{2,1,0:T(8,128)} all-to-all(f32[16,64,128]{2,1,0:T(8,128)S(1)} %copy.17), channel_id=1, replica_groups=mesh['frame'=16,'row'=16] {'frame'}, dimensions={0} | all-to-all | bytes 1048576 | tf_op jit(solution)/shard_map/all_to_all | solution.py:41
  99.0 1.1 reduce_sum.103
  100.1 13.7 %all_to_all.41 = f32[16,32,128]{2,1,0:T(8,128)S(1)} all-to-all(f32[16,32,128]{2,1,0:T(8,128)S(1)} %broadcast_in_dim.9), channel_id=1, replica_groups=mesh['frame'=16,'row'=16] {'frame'}, dimensions={0} | all-to-all | bytes 524288 | tf_op jit(solution)/shard_map/all_to_all | solution.py:27
  113.8 1.9 collective-permute-start.4
  115.7 7.5 %collective-permute-start.5 = (f32[8,2048]{1,0:T(8,128)S(1)}, f32[8,2048]{1,0:T(8,128)S(1)}, u32[]{:S(2)}, u32[]{:S(2)}) collective-permute-start(f32[8,2048]{1,0:T(8,128)S(1)} %get-tuple-element.30), channel_id=1, source_target_pairs={{1,0},{2,1},{3,2},{4,3},{5,4},{6,5},{7,6},{8,7},{9,8},{10,9},{11,1... | collective-permute-start | bytes 196616 | tf_op jit(solution)/shard_map/ppermute | solution.py:60
  123.3 1.6 collective-permute-done.5
  124.9 0.2 broadcast_multiply_fusion.1
  125.1 0.9 slice_add_fusion.8
  126.0 0.2 slice_add_fusion.94
  126.3 0.2 fusion.28
  126.5 1.4 fusion.24
  128.0 2.8 %broadcast_multiply_fusion.4 = (f32[4,40,2048]{2,1,0:T(8,128)S(1)}, f32[4,40,2048]{2,1,0:T(8,128)S(1)}) fusion(f32[40]{0:T(128)S(1)} %and_convert_fusion, f32[40,2048]{1,0:T(8,128)S(1)} %get-tuple-element.17, f32[4,40,2048]{2,1,0:T(8,128)S(1)} %get-tuple-element.21, f32[40,2048]{1,0:T(8,128)S(1)} %get-tuple-element.18, ...), kind=kLoop, calls=%fused_computation.153 | loop fusion | flops 4259840 | bytes 6226080 | tf_op jit(solution)/shard_map/mul | solution.py:125
  130.8 0.3 subtract_multiply_fusion.1
  131.1 0.7 slice_add_fusion.47
  131.9 0.7 slice_add_fusion.55
  132.6 0.5 copy-done.2
  133.1 4.5 %multiply_reduce_fusion.1 = (f32[32,2048]{1,0:T(8,128)S(1)}, f32[32,2048]{1,0:T(8,128)S(1)}) fusion(f32[4,32,2048]{2,1,0:T(8,128)S(1)} %copy-done.2, f32[4,32,2048]{2,1,0:T(8,128)S(1)} %slice_add_fusion.47, f32[32,2048]{1,0:T(8,128)S(1)} %copy_bitcast_fusion.2, f32[32,2048]{1,0:T(8,128)S(1)} %broadcast_multiply_fusion.7, f32[4,32,2048]{2,1,0:T(8,128)S(1)} %slice_add_fusion.55), kind=kLoop, calls=%fused_computation.119 | loop fusion | flops 7208960 | bytes 4194304 | tf_op jit(solution)/shard_map/reduce_sum | solution.py:130
  138.0 20.6 %all_to_all.42 = f32[16,64,128]{2,1,0:T(8,128)} all-to-all(f32[16,64,128]{2,1,0:T(8,128)S(1)} %copy.19), channel_id=1, replica_groups=mesh['frame'=16,'row'=16] {'frame'}, dimensions={0} | all-to-all | bytes 1048576 | tf_op jit(solution)/shard_map/all_to_all | solution.py:41
  158.5 1.1 reduce_sum.106
  159.7 13.7 %all_to_all.43 = f32[16,32,128]{2,1,0:T(8,128)S(1)} all-to-all(f32[16,32,128]{2,1,0:T(8,128)S(1)} %broadcast_in_dim.10), channel_id=1, replica_groups=mesh['frame'=16,'row'=16] {'frame'}, dimensions={0} | all-to-all | bytes 524288 | tf_op jit(solution)/shard_map/all_to_all | solution.py:27
  173.4 1.9 collective-permute-start.6
  175.3 7.5 %collective-permute-start.7 = (f32[8,2048]{1,0:T(8,128)S(1)}, f32[8,2048]{1,0:T(8,128)S(1)}, u32[]{:S(2)}, u32[]{:S(2)}) collective-permute-start(f32[8,2048]{1,0:T(8,128)S(1)} %get-tuple-element.28), channel_id=1, source_target_pairs={{1,0},{2,1},{3,2},{4,3},{5,4},{6,5},{7,6},{8,7},{9,8},{10,9},{11,1... | collective-permute-start | bytes 196616 | tf_op jit(solution)/shard_map/ppermute | solution.py:60
  182.9 1.5 collective-permute-done.7
  184.5 0.2 broadcast_multiply_fusion
  184.7 0.9 slice_add_fusion
  185.6 0.2 slice_add_fusion.79
  185.9 0.2 fusion.27
  186.1 1.4 fusion.26
  187.6 2.8 %broadcast_multiply_fusion.3 = (f32[4,40,2048]{2,1,0:T(8,128)S(1)}, f32[4,40,2048]{2,1,0:T(8,128)S(1)}) fusion(f32[40]{0:T(128)S(1)} %and_convert_fusion, f32[40,2048]{1,0:T(8,128)S(1)} %get-tuple-element.13, f32[4,40,2048]{2,1,0:T(8,128)S(1)} %get-tuple-element.21, f32[40,2048]{1,0:T(8,128)S(1)} %get-tuple-element.14, ...), kind=kLoop, calls=%fused_computation.152 | loop fusion | flops 4259840 | bytes 6226080 | tf_op jit(solution)/shard_map/mul | solution.py:125
  190.3 0.3 subtract_multiply_fusion
  190.7 0.7 slice_add_fusion.31
  191.5 0.7 slice_add_fusion.39
  192.2 0.5 copy-done.3
  192.7 4.6 %multiply_reduce_fusion = (f32[32,2048]{1,0:T(8,128)S(1)}, f32[32,2048]{1,0:T(8,128)S(1)}) fusion(f32[4,32,2048]{2,1,0:T(8,128)S(1)} %copy-done.3, f32[4,32,2048]{2,1,0:T(8,128)S(1)} %slice_add_fusion.31, f32[32,2048]{1,0:T(8,128)S(1)} %copy_bitcast_fusion.1, f32[32,2048]{1,0:T(8,128)S(1)} %broadcast_multiply_fusion.7, f32[4,32,2048]{2,1,0:T(8,128)S(1)} %slice_add_fusion.39), kind=kLoop, calls=%fused_computation.107 | loop fusion | flops 7208960 | bytes 4194304 | tf_op jit(solution)/shard_map/reduce_sum | solution.py:130
  197.6 18.8 %all_to_all.44 = f32[16,64,128]{2,1,0:T(8,128)S(1)} all-to-all(f32[16,64,128]{2,1,0:T(8,128)S(1)} %copy.21), channel_id=1, replica_groups=mesh['frame'=16,'row'=16] {'frame'}, dimensions={0} | all-to-all | bytes 1048576 | tf_op jit(solution)/shard_map/all_to_all | solution.py:41
  216.5 13.7 %all_to_all.45 = f32[16,32,128]{2,1,0:T(8,128)S(1)} all-to-all(f32[16,32,128]{2,1,0:T(8,128)S(1)} %broadcast_in_dim.11), channel_id=1, replica_groups=mesh['frame'=16,'row'=16] {'frame'}, dimensions={0} | all-to-all | bytes 524288 | tf_op jit(solution)/shard_map/all_to_all | solution.py:27
  230.1 0.7 copy_bitcast_fusion
  (60 shorter events, 1.8 us)
Async XLA Ops:
  0.0 13.2 %copy-start = (f32[4,32,2048]{2,1,0:T(8,128)S(1)}, f32[4,32,2048]{2,1,0:T(8,128)}, u32[]{:S(2)}) copy-start(f32[4,32,2048]{2,1,0:T(8,128)} %param.1) | copy-start | bytes 3145732
  1.9 11.3 %collective-permute-start.2 = (f32[4,8,2048]{2,1,0:T(8,128)S(1)}, f32[4,8,2048]{2,1,0:T(8,128)S(1)}, u32[]{:S(2)}, u32[]{:S(2)}) collective-permute-start(f32[4,8,2048]{2,1,0:T(8,128)S(1)} %get-tuple-element.25), channel_id=1, source_target_pairs={{0,1},{1,2},{2,3},{3,4},{4,5},{5,6},{6,7},{7,8},{8,9},{9,10},{10,1... | collective-permute-start | bytes 786440 | tf_op jit(solution)/shard_map/ppermute | solution.py:59
  14.2 20.0 %all-to-all-start = ((f32[16,2,2048]{2,1,0:T(2,128)}), f32[16,2,2048]{2,1,0:T(2,128)S(1)}, u32[]{:S(2)}, u32[]{:S(2)}) async-start(f32[16,2,2048]{2,1,0:T(2,128)} %reshape.144), calls=%async_computation | async-start | bytes 524288 | tf_op jit(solution)/shard_map/all_to_all | solution.py:41
  23.4 16.0 %collective-permute-start.3 = (f32[4,8,2048]{2,1,0:T(8,128)}, f32[4,8,2048]{2,1,0:T(8,128)S(1)}, u32[]{:S(2)}, u32[]{:S(2)}) collective-permute-start(f32[4,8,2048]{2,1,0:T(8,128)} %get-tuple-element.24), channel_id=1, source_target_pairs={{1,0},{2,1},{3,2},{4,3},{5,4},{6,5},{7,6},{8,7},{9,8},{10,9},{11,1... | collective-permute-start | bytes 786440 | tf_op jit(solution)/shard_map/ppermute | solution.py:60
  35.1 15.3 %all-to-all-start.1 = ((f32[16,2,2048]{2,1,0:T(2,128)}), f32[16,2,2048]{2,1,0:T(2,128)}, u32[]{:S(2)}, u32[]{:S(2)}) async-start(f32[16,2,2048]{2,1,0:T(2,128)} %broadcast_in_dim.8), calls=%async_computation.1 | async-start | bytes 524288 | tf_op jit(solution)/shard_map/all_to_all | solution.py:27
  39.4 0.7 copy-start.7
  52.1 12.6 %collective-permute-start = (f32[8,2048]{1,0:T(8,128)}, f32[8,2048]{1,0:T(8,128)S(1)}, u32[]{:S(2)}, u32[]{:S(2)}) collective-permute-start(f32[8,2048]{1,0:T(8,128)} %slice.903), channel_id=1, source_target_pairs={{0,1},{1,2},{2,3},{3,4},{4,5},{5,6},{6,7},{7,8},{8,9},{9,10},{10,1... | collective-permute-start | bytes 196616 | tf_op jit(solution)/shard_map/ppermute | solution.py:59
  57.2 10.6 %copy-start.5 = (f32[32,2048]{1,0:T(8,128)}, f32[32,2048]{1,0:T(8,128)S(1)}, u32[]{:S(2)}) copy-start(f32[32,2048]{1,0:T(8,128)S(1)} %div.74) | copy-start | bytes 786436
  57.2 9.1 %collective-permute-start.1 = (f32[8,2048]{1,0:T(8,128)S(1)}, f32[8,2048]{1,0:T(8,128)S(1)}, u32[]{:S(2)}, u32[]{:S(2)}) collective-permute-start(f32[8,2048]{1,0:T(8,128)S(1)} %slice.905), channel_id=1, source_target_pairs={{1,0},{2,1},{3,2},{4,3},{5,4},{6,5},{7,6},{8,7},{9,8},{10,9},{11,1... | collective-permute-start | bytes 196616 | tf_op jit(solution)/shard_map/ppermute | solution.py:60
  68.1 1.4 copy-start.4
  75.5 1.6 copy-start.1
  75.5 1.6 copy-start.6
  113.8 9.4 %collective-permute-start.4 = (f32[8,2048]{1,0:T(8,128)S(1)}, f32[8,2048]{1,0:T(8,128)S(1)}, u32[]{:S(2)}, u32[]{:S(2)}) collective-permute-start(f32[8,2048]{1,0:T(8,128)S(1)} %get-tuple-element.31), channel_id=1, source_target_pairs={{0,1},{1,2},{2,3},{3,4},{4,5},{5,6},{6,7},{7,8},{8,9},{9,10},{10,1... | collective-permute-start | bytes 196616 | tf_op jit(solution)/shard_map/ppermute | solution.py:59
  115.7 9.1 %collective-permute-start.5 = (f32[8,2048]{1,0:T(8,128)S(1)}, f32[8,2048]{1,0:T(8,128)S(1)}, u32[]{:S(2)}, u32[]{:S(2)}) collective-permute-start(f32[8,2048]{1,0:T(8,128)S(1)} %get-tuple-element.30), channel_id=1, source_target_pairs={{1,0},{2,1},{3,2},{4,3},{5,4},{6,5},{7,6},{8,7},{9,8},{10,9},{11,1... | collective-permute-start | bytes 196616 | tf_op jit(solution)/shard_map/ppermute | solution.py:60
  131.9 1.2 copy-start.2
  173.4 9.5 %collective-permute-start.6 = (f32[8,2048]{1,0:T(8,128)S(1)}, f32[8,2048]{1,0:T(8,128)S(1)}, u32[]{:S(2)}, u32[]{:S(2)}) collective-permute-start(f32[8,2048]{1,0:T(8,128)S(1)} %get-tuple-element.29), channel_id=1, source_target_pairs={{0,1},{1,2},{2,3},{3,4},{4,5},{5,6},{6,7},{7,8},{8,9},{9,10},{10,1... | collective-permute-start | bytes 196616 | tf_op jit(solution)/shard_map/ppermute | solution.py:59
  175.3 9.1 %collective-permute-start.7 = (f32[8,2048]{1,0:T(8,128)S(1)}, f32[8,2048]{1,0:T(8,128)S(1)}, u32[]{:S(2)}, u32[]{:S(2)}) collective-permute-start(f32[8,2048]{1,0:T(8,128)S(1)} %get-tuple-element.28), channel_id=1, source_target_pairs={{1,0},{2,1},{3,2},{4,3},{5,4},{6,5},{7,6},{8,7},{9,8},{10,9},{11,1... | collective-permute-start | bytes 196616 | tf_op jit(solution)/shard_map/ppermute | solution.py:60
  191.4 1.2 copy-start.3
where the time goes:
time: 234 us; the launch traced here: 231 us
  blocking collectives  97.4 us (42%)
  other arithmetic  46.3 us (20%)
  starting transfers between devices  45.4 us (19%)
  waiting for transfers between devices  33.2 us (14%)
  local copies, waits for them, and re-layouts  7.81 us (3%)
    all_to_all x3, blocking collectives, summed_on_arrival(): parts = lax.all_to_all(cut_along(x, dim, count), axis, 0, 0, tiled=True)  56.4 us
    all_to_all x3, blocking collectives, copy_for_each(): return lax.all_to_all(copies, axis, split_axis=0, concat_axis=0, tiled=True)  41.1 us
    ppermute x4, starting transfers between devices, with_halo(): after = lax.ppermute(initial, axis, down)  24.3 us
    reduce_sum x3, other arithmetic, shards(): weighted = jnp.sum(weight * frames, axis=0)  13.6 us
    add x15, other arithmetic, row_sum(): total = total + field[..., offset:offset + length, :]  11.7 us
    mul x3, other arithmetic, shards(): slope_rows = slope * inside  11.2 us
    all_to_all x1, waiting for transfers between devices, copy_for_each(): return lax.all_to_all(copies, axis, split_axis=0, concat_axis=0, tiled=True)  10.2 us
    ppermute x4, waiting for transfers between devices, with_halo(): before = lax.ppermute(last, axis, up)  9.38 us
  transfers between devices with their start and end apart: 10, of which 6 were waited for; matrix products, arithmetic and copies ran while one was open for 2% of the time, Pallas kernels for 0%

commit v1 on v0

v1 whole, which is shorter than its diff:
```python
import functools

import jax
import jax.numpy as jnp
from jax import lax
from jax.experimental import pallas as pl
from jax.experimental.pallas import tpu as pltpu
from jax.sharding import PartitionSpec as P

FRAMES = 64
ROUNDS = 3
GUIDE_EPS = 0.05
CAUCHY_SCALE = 0.5

LANES = 128
ROWS = 32
WIN = ROWS + 16
PITCH = 56
HALF = 64
PAIR = 16
CHUNK = 8
MESH = pl.DeviceIdType.MESH

WAYS = ((0, -1), (0, 1), (-1, 0), (1, 0), (-1, -1), (-1, 1), (1, -1), (1, 1))


def snake(i):
    z = i // 2
    return z * 2 + (i % 2 + z) % 2


def windows(a, count):
    two = [a[i] + a[i + 1] for i in range(count + 6)]
    four = [two[i] + two[i + 2] for i in range(count + 4)]
    return [(four[i] + four[i + 4]) + a[i + 8] for i in range(count)]


def down_sum(x):
    n = x.shape[0]
    two = x + pltpu.roll(x, n - 1, 0)
    four = two + pltpu.roll(two, n - 2, 0)
    eight = four + pltpu.roll(four, n - 4, 0)
    return eight[: n - 8] + x[8:]


def across_sum(x):
    n = x.shape[1]
    two = x + pltpu.roll(x, n - 1, 1)
    four = two + pltpu.roll(two, n - 2, 1)
    eight = four + pltpu.roll(four, n - 4, 1)
    return eight + pltpu.roll(x, n - 8, 1)


def window_count(place, limit):
    lower = jnp.maximum(place - 4, 0)
    upper = jnp.minimum(place + 4, limit - 1)
    return jnp.maximum(upper - lower + 1, 1).astype(jnp.float32)


def kernel(
    nf, nr, frames, out, recv, flat, tf, rowbox, mean, area, slope, offset, box1, box2,
    table, est, fin, own_sem, a2a_send, a2a_recv, row_send, row_recv, col_send,
    col_recv, est_send, est_recv, fin_send, fin_recv,
):
    per = FRAMES // nf
    f = lax.axis_index("frame")
    r = lax.axis_index("row")
    c = snake(f)
    up, down = r > 0, r < nr - 1
    left, right = c > 0, c < nf - 1
    left_f = snake(jnp.maximum(c - 1, 0))
    right_f = snake(jnp.minimum(c + 1, nf - 1))

    def there(dr, dc):
        ok = None
        for test, step in ((up, dr == -1), (down, dr == 1), (left, dc == -1), (right, dc == 1)):
            if step:
                ok = test if ok is None else jnp.logical_and(ok, test)
        return ok

    def device(dr, dc):
        return {
            "frame": f if dc == 0 else (left_f if dc < 0 else right_f),
            "row": jnp.clip(r + dr, 0, nr - 1),
        }

    own = pltpu.make_async_copy(
        frames.at[:, :, pl.ds(pl.multiple_of(c * LANES, LANES), LANES)],
        recv.at[pl.ds(f * per, per), pl.ds(8, ROWS), :],
        own_sem,
    )
    own.start()

    est[...] = jnp.zeros_like(est)

    @pl.when(jnp.logical_not(up))
    def _():
        recv[:, 0:8, :] = jnp.zeros((FRAMES, 8, LANES), jnp.float32)

    @pl.when(jnp.logical_not(down))
    def _():
        recv[:, 40:48, :] = jnp.zeros((FRAMES, 8, LANES), jnp.float32)

    @pl.when(jnp.logical_not(left))
    def _():
        tf[:, 0:8, :] = jnp.zeros((32, 8, LANES), jnp.float32)

    @pl.when(jnp.logical_not(right))
    def _():
        tf[:, 136:144, :] = jnp.zeros((32, 8, LANES), jnp.float32)

    barrier = pltpu.get_barrier_semaphore()

    @pl.loop(1, nf)
    def _(s):
        pl.semaphore_signal(
            barrier, inc=1, device_id={"frame": (f + s) % nf, "row": r}, device_id_type=MESH
        )

    others = jnp.int32(nf - 1)
    for dr, dc in WAYS:
        if dr == 0:
            continue

        @pl.when(there(dr, dc))
        def _(dr=dr, dc=dc):
            pl.semaphore_signal(barrier, inc=1, device_id=device(dr, dc), device_id_type=MESH)

        others = others + there(dr, dc).astype(jnp.int32)
    pl.semaphore_wait(barrier, others)

    def block(k, peer, to):
        return pltpu.make_async_remote_copy(
            src_ref=frames.at[
                :, pl.ds(k * CHUNK, CHUNK), pl.ds(pl.multiple_of(snake(to) * LANES, LANES), LANES)
            ],
            dst_ref=recv.at[pl.ds(peer * per, per), pl.ds(8 + k * CHUNK, CHUNK), :],
            send_sem=a2a_send.at[k, to],
            recv_sem=a2a_recv.at[k, peer],
            device_id={"frame": to, "row": r},
            device_id_type=MESH,
        )

    def step_of(s):
        d = (s + 1) // 2
        return jnp.where(s % 2 == 1, d, nf - d)

    order = (0, 3, 1, 2)
    for k in order:

        @pl.loop(1, nf)
        def _(s, k=k):
            block(k, f, (f + step_of(s)) % nf).start()

    def arrived(k):
        @pl.loop(1, nf)
        def _(s):
            peer = (f + s) % nf
            block(k, peer, peer).wait_recv()

    def edge(dr):
        at, to = (8, 40) if dr < 0 else (32, 0)
        i = 0 if dr < 0 else 1
        return pltpu.make_async_remote_copy(
            src_ref=recv.at[:, pl.ds(at, 8), :],
            dst_ref=recv.at[:, pl.ds(to, 8), :],
            send_sem=row_send.at[i],
            recv_sem=row_recv.at[i],
            device_id=device(dr, 0),
            device_id_type=MESH,
        )

    lane = lax.broadcasted_iota(jnp.int32, (8, LANES), 1)
    second = jnp.where(lane >= HALF, PAIR, 0)
    height, width = nr * ROWS, nf * LANES
    place_r = r * ROWS - 4 + lax.broadcasted_iota(jnp.int32, (40, 2 * LANES), 0)
    place_c = c * LANES - 4 + lax.broadcasted_iota(jnp.int32, (40, 2 * LANES), 1)
    cells = window_count(place_r, height) * window_count(place_c, width)
    inside = jnp.where(
        (place_r >= 0) & (place_r < height) & (place_c >= 0) & (place_c < width), 1.0, 0.0
    )
    share = 1.0 / cells

    def keep(top, mid, low):
        both = jnp.concatenate([top, mid, low], axis=0)
        table[0:LANES, :] = both[:, 0:LANES].T
        table[LANES : LANES + 16, :] = both[:, LANES : 2 * LANES].T[0:16]

    def spread(x, row):
        idx = jnp.broadcast_to((second + row)[0:1], x.shape)
        return jnp.take_along_axis(x, idx, axis=1, mode="promise_in_bounds")

    zeros48 = jnp.zeros((WIN, 2 * LANES), jnp.float32)
    keep(zeros48, share * inside, share)

    @pl.loop(0, 24)
    def _(i):
        area[i] = spread(table[0:136, :], 48 + i)

    own.wait()
    arrived(0)

    @pl.when(up)
    def _():
        edge(-1).start()

    arrived(3)

    @pl.when(down)
    def _():
        edge(1).start()

    def lay(at):
        @pl.loop(0, FRAMES)
        def _(p):
            flat[pl.ds(pl.multiple_of(p * PITCH + at, 8), 8), :] = recv[p, at : at + 8, :]

    def turn(q):
        @pl.loop(0, 8)
        def _(i):
            row = q * 8 + i
            a = flat[pl.ds(row, FRAMES, stride=PITCH), :]
            b = flat[pl.ds(row + PAIR, FRAMES, stride=PITCH), :]
            tf[row, 8:136, :] = jnp.concatenate([a, b], axis=0).T

    def side(q, dc):
        at, to = (8, 136) if dc < 0 else (128, 0)
        i = 0 if dc < 0 else 1
        return pltpu.make_async_remote_copy(
            src_ref=tf.at[pl.ds(q * 8, 8), pl.ds(at, 8), :],
            dst_ref=tf.at[pl.ds(q * 8, 8), pl.ds(to, 8), :],
            send_sem=col_send.at[i, q],
            recv_sem=col_recv.at[i, q],
            device_id=device(0, dc),
            device_id_type=MESH,
        )

    def turned(q):
        turn(q)
        for dc in (-1, 1):

            @pl.when(there(0, dc))
            def _(dc=dc):
                side(q, dc).start()

    lay(8)
    lay(32)
    arrived(1)
    lay(16)
    turned(2)

    @pl.when(up)
    def _():
        edge(1).wait_recv()

    lay(0)
    turned(0)
    arrived(2)
    lay(24)
    turned(1)

    @pl.when(down)
    def _():
        edge(-1).wait_recv()

    lay(40)
    turned(3)

    def part(e, way):
        dr, dc = WAYS[way]
        at, size, to = {0: (8, ROWS, 8), -1: (8, 8, 40), 1: (32, 8, 0)}[dr]
        return pltpu.make_async_remote_copy(
            src_ref=est.at[e, 1, pl.ds(at, size), :],
            dst_ref=est.at[e, 1 - dc, pl.ds(to, size), :],
            send_sem=est_send.at[e, way],
            recv_sem=est_recv.at[e, way],
            device_id=device(dr, dc),
            device_id_type=MESH,
        )

    def give(e):
        for way, (dr, dc) in enumerate(WAYS):

            @pl.when(there(dr, dc))
            def _(way=way):
                part(e, way).start()

    def take(e):
        for way, (dr, dc) in enumerate(WAYS):

            @pl.when(there(-dr, -dc))
            def _(way=way):
                part(e, way).wait_recv()

    total = lax.fori_loop(
        0, FRAMES, lambda p, t: t + recv[p, 8:40, :], jnp.zeros((ROWS, LANES), jnp.float32)
    )
    est[0, 1, 8:40, :] = total / FRAMES
    give(0)

    for dc in (-1, 1):

        @pl.when(there(0, -dc))
        def _(dc=dc):
            for q in range(4):
                side(q, dc).wait_recv()

    @pl.loop(0, 18)
    def _(j):
        at = pl.ds(pl.multiple_of(j * 8, 8), 8)
        for i, s in enumerate(windows([tf[i, at, :] for i in range(32)], 24)):
            rowbox[i, at, :] = s

    @pl.loop(0, 24)
    def _(i):
        mean[i] = down_sum(rowbox[i]) * area[i]

    for e in range(ROUNDS):
        take(e)
        near = jnp.concatenate([est[e, 0], est[e, 1], est[e, 2]], axis=1)
        guide = pltpu.roll(near, 3 * LANES - 120, 1)[:, 0 : 2 * LANES]

        def smooth(x):
            x = across_sum(x)
            two = x[0:47] + x[1:48]
            four = two[0:45] + two[2:47]
            return (four[0:40] + four[4:44] + x[8:48]) / cells

        mean_guide = smooth(guide)
        variance = smooth(guide * guide) - mean_guide * mean_guide
        keep(guide, mean_guide, inside / (variance + GUIDE_EPS))

        @pl.loop(0, 18)
        def _(j):
            at = pl.ds(pl.multiple_of(j * 8, 8), 8)
            t = table[at, :]
            products = [tf[i, at, :] * spread(t, i) for i in range(32)]
            for i, s in enumerate(windows(products, 24)):
                rowbox[i, at, :] = s

        @pl.loop(0, 24)
        def _(i):
            t = table[0:136, :]
            guided = spread(t, 48 + i)
            m = mean[i]
            sl = (down_sum(rowbox[i]) * area[i] - guided * m) * spread(t, 88 + i)
            slope[i] = sl
            offset[i] = m - sl * guided

        @pl.loop(0, 17)
        def _(j):
            at = pl.ds(pl.multiple_of(j * 8, 8), 8)
            for src, dst in ((slope, box1), (offset, box2)):
                for i, s in enumerate(windows([src[i, at, :] for i in range(24)], 16)):
                    dst[i, at, :] = s

        wide = lax.broadcasted_iota(jnp.int32, (LANES, LANES), 1)
        low = wide < HALF

        def weigh(i, acc):
            center = spread(table[8:136, :], 8 + i)
            filtered = (down_sum(box1[i]) * center + down_sum(box2[i])) * area[i + 4, 4:132, :]
            gap = (filtered - center) * (1.0 / CAUCHY_SCALE)
            weight = 1.0 / (1.0 + gap * gap)
            for x, at in ((weight, 0), (weight * tf[i + 8, 8:136, :], 16)):
                a = jnp.sum(jnp.where(low, x, 0.0), axis=1, keepdims=True)
                b = jnp.sum(jnp.where(low, 0.0, x), axis=1, keepdims=True)
                acc = jnp.where(wide == at + i, a, acc)
                acc = jnp.where(wide == HALF + at + i, b, acc)
            return acc

        acc = lax.fori_loop(0, PAIR, weigh, jnp.zeros((LANES, LANES), jnp.float32)).T
        new = jnp.concatenate(
            [acc[16:32] / acc[0:16], acc[80:96] / acc[64:80]], axis=0
        )
        if e < ROUNDS - 1:
            est[e + 1, 1, 8:40, :] = new
            give(e + 1)
        else:
            fin[...] = new

    def final(of, to):
        return pltpu.make_async_remote_copy(
            src_ref=fin,
            dst_ref=out.at[:, pl.ds(pl.multiple_of(snake(of) * LANES, LANES), LANES)],
            send_sem=fin_send.at[to],
            recv_sem=fin_recv.at[of],
            device_id={"frame": to, "row": r},
            device_id_type=MESH,
        )

    @pl.loop(1, nf)
    def _(s):
        final(f, (f + step_of(s)) % nf).start()

    mine = pltpu.make_async_copy(
        fin, out.at[:, pl.ds(pl.multiple_of(c * LANES, LANES), LANES)], own_sem
    )
    mine.start()

    for k in order:

        @pl.loop(1, nf)
        def _(s, k=k):
            block(k, f, (f + s) % nf).wait_send()

    for dr in (-1, 1):

        @pl.when(there(dr, 0))
        def _(dr=dr):
            edge(dr).wait_send()

    for dc in (-1, 1):

        @pl.when(there(0, dc))
        def _(dc=dc):
            for q in range(4):
                side(q, dc).wait_send()

    for e in range(ROUNDS):
        for way, (dr, dc) in enumerate(WAYS):

            @pl.when(there(dr, dc))
            def _(e=e, way=way):
                part(e, way).wait_send()

    @pl.loop(1, nf)
    def _(s):
        peer = (f + s) % nf
        final(peer, peer).wait_recv()
        final(f, peer).wait_send()

    mine.wait()


def merge(nf, nr, frames):
    f32 = jnp.float32
    dma = pltpu.SemaphoreType.DMA
    return pl.pallas_call(
        functools.partial(kernel, nf, nr),
        out_shape=jax.ShapeDtypeStruct((ROWS, nf * LANES), f32),
        in_specs=[pl.BlockSpec(memory_space=pl.ANY)],
        out_specs=pl.BlockSpec(memory_space=pl.ANY),
        scratch_shapes=[
            pltpu.VMEM((FRAMES, WIN, LANES), f32),
            pltpu.VMEM((FRAMES * PITCH, LANES), f32),
            pltpu.VMEM((32, 144, LANES), f32),
            pltpu.VMEM((24, 144, LANES), f32),
            pltpu.VMEM((24, 136, LANES), f32),
            pltpu.VMEM((24, 136, LANES), f32),
            pltpu.VMEM((24, 136, LANES), f32),
            pltpu.VMEM((24, 136, LANES), f32),
            pltpu.VMEM((16, 136, LANES), f32),
            pltpu.VMEM((16, 136, LANES), f32),
            pltpu.VMEM((144, LANES), f32),
            pltpu.VMEM((ROUNDS, 3, WIN, LANES), f32),
            pltpu.VMEM((ROWS, LANES), f32),
            dma,
            dma((4, nf)),
            dma((4, nf)),
            dma((2,)),
            dma((2,)),
            dma((2, 4)),
            dma((2, 4)),
            dma((ROUNDS, 8)),
            dma((ROUNDS, 8)),
            dma((nf,)),
            dma((nf,)),
        ],
        compiler_params=pltpu.CompilerParams(collective_id=0, has_side_effects=True),
        name="merge",
    )(frames)


def solution(mesh):
    return jax.shard_map(
        functools.partial(merge, mesh.shape["frame"], mesh.shape["row"]),
        mesh=mesh,
        in_specs=(P("frame", "row", None),),
        out_specs=P("row", None),
        check_vma=False,
    )
```

time: 234 us -> 93.8 us (0.40); the launches traced: 231 us -> 93.7 us
  blocking collectives: 97.4 us -> 0 us
  Pallas kernels: 0 us -> 92 us
  other arithmetic: 46.3 us -> 0 us
  starting transfers between devices: 45.4 us -> 0 us
  waiting for transfers between devices: 33.2 us -> 0 us
  local copies, waits for them, and re-layouts: 7.81 us -> 1.67 us
    all_to_all x6 -> x0, blocking collectives: 97.4 us -> none  [the longest x3 56.4 us: summed_on_arrival(): parts = lax.all_to_all(cut_along(x, dim, count), axis, 0, 0, tiled=True)]
    pallas_call x0 -> x1, Pallas kernels: none -> 92 us  [merge(): pl.pallas_call(functools.partial(kernel, nf, nr), out_shape=jax.ShapeDtyp...]
    ppermute x8 -> x0, starting transfers between devices: 32 us -> none  [the longest x4 24.3 us: with_halo(): after = lax.ppermute(initial, axis, down)]
    all_to_all x2 -> x0, waiting for transfers between devices: 19 us -> none  [the longest x1 10.2 us: copy_for_each(): return lax.all_to_all(copies, axis, split_axis=0, concat_axis=0, tiled=True)]
    add x18 -> x0, other arithmetic: 16 us -> none  [the longest x15 11.7 us: row_sum(): total = total + field[..., offset:offset + length, :]]
    reduce_sum x7 -> x0, other arithmetic: 15.9 us -> none  [the longest x3 13.6 us: shards(): weighted = jnp.sum(weight * frames, axis=0)]
    ppermute x8 -> x0, waiting for transfers between devices: 14.2 us -> none  [the longest x4 9.38 us: with_halo(): before = lax.ppermute(last, axis, up)]
    all_to_all x2 -> x0, starting transfers between devices: 13.4 us -> none  [the longest x1 9.2 us: summed_on_arrival(): parts = lax.all_to_all(cut_along(x, dim, count), axis, 0, 0, tiled=True)]
  transfers between devices with their start and end apart: 10 -> 0, of which waited for: 6 -> 0; matrix products, arithmetic and copies ran while one was open for 2% -> 0% of each run, Pallas kernels for 0% -> 0%
where the time goes in v1:
time: 93.8 us; the launch traced here: 93.7 us
  Pallas kernels  92 us (98%)
  local copies, waits for them, and re-layouts  1.67 us (2%)
    pallas_call x1, Pallas kernels, merge(): pl.pallas_call(functools.partial(kernel, nf, nr), out_shape=jax.ShapeDtyp...  92 us

profile of v1, /device:TPU:4, one launch (start us, length us, event | category | flops | bytes accessed | tf_op | source)
XLA Modules:
  0.0 93.7 jit_solution(1037089960867052597)
XLA Ops:
  0.0 92.0 %merge.1 = f32[32,2048]{1,0:T(8,128)} custom-call(f32[4,32,2048]{2,1,0:T(8,128)} %frames.1), custom_call_target="tpu_custom_call" | custom-call | tf_op jit(solution)/shard_map/merge/pallas_call | solution.py:439
  92.0 1.7 %copy.3 = f32[32,2048]{1,0:T(8,128)} copy(f32[32,2048]{1,0:T(8,128)} %merge.1) | data formatting | bytes 524288

commit v2 on v1

--- a/solution.py
+++ b/solution.py
@@ -51,6 +51,20 @@
     return eight + pltpu.roll(x, n - 8, 1)
 
 
+def thirds(x):
+    high = x.astype(jnp.bfloat16)
+    rest = x - high.astype(jnp.float32)
+    mid = rest.astype(jnp.bfloat16)
+    return high, mid, (rest - mid.astype(jnp.float32)).astype(jnp.bfloat16)
+
+
+def stacked(*arrays):
+    rows = [t.astype(jnp.float32) for a in arrays for t in thirds(a)]
+    spare = 256 - sum(t.shape[0] for t in rows)
+    rows.append(jnp.zeros((spare, rows[0].shape[1]), jnp.float32))
+    return jnp.concatenate(rows, axis=0).astype(jnp.bfloat16).T[0:144]
+
+
 def window_count(place, limit):
     lower = jnp.maximum(place - 4, 0)
     upper = jnp.minimum(place + 4, limit - 1)
@@ -59,7 +73,7 @@
 
 def kernel(
     nf, nr, frames, out, recv, flat, tf, rowbox, mean, area, slope, offset, box1, box2,
-    table, est, fin, own_sem, a2a_send, a2a_recv, row_send, row_recv, col_send,
+    table, gb, guide_t, stat_t, pick_g, pick_s, pick_w, est, fin, own_sem, a2a_send, a2a_recv, row_send, row_recv, col_send,
     col_recv, est_send, est_recv, fin_send, fin_recv,
 ):
     per = FRAMES // nf
@@ -197,6 +211,28 @@
     def _(i):
         area[i] = spread(table[0:136, :], 48 + i)
 
+    k = lax.broadcasted_iota(jnp.int32, (256, 256), 0)
+    n = lax.broadcasted_iota(jnp.int32, (256, 256), 1)
+    side_n, half_n = n // LANES, jnp.where(n % LANES >= HALF, PAIR, 0)
+    row_g = jnp.where(k < 144, k % 48, 255) - half_n - side_n
+    row_s = jnp.where(k // 120 == side_n, k % 40, 255) - half_n
+
+    @pl.loop(0, 16)
+    def _(q):
+        pick_g[q] = jnp.where(row_g == 2 * q, 1.0, 0.0).astype(jnp.bfloat16)
+
+    @pl.loop(0, 24)
+    def _(i):
+        pick_s[i] = jnp.where(row_s == i, 1.0, 0.0).astype(jnp.bfloat16)
+
+    k = lax.broadcasted_iota(jnp.int32, (384, LANES), 0) % LANES
+    n = lax.broadcasted_iota(jnp.int32, (384, LANES), 1)
+    row_w = n - jnp.where(k >= HALF, HALF, 0) - jnp.where(k % HALF >= 32, 0, 16)
+
+    @pl.loop(0, PAIR)
+    def _(i):
+        pick_w[i] = jnp.where(row_w == i, 1.0, 0.0).astype(jnp.bfloat16)
+
     own.wait()
     arrived(0)
 
@@ -211,12 +247,12 @@
         edge(1).start()
 
     def lay(at):
-        @pl.loop(0, FRAMES)
+        @pl.loop(0, FRAMES, unroll=8)
         def _(p):
             flat[pl.ds(pl.multiple_of(p * PITCH + at, 8), 8), :] = recv[p, at : at + 8, :]
 
     def turn(q):
-        @pl.loop(0, 8)
+        @pl.loop(0, 8, unroll=8)
         def _(i):
             row = q * 8 + i
             a = flat[pl.ds(row, FRAMES, stride=PITCH), :]
@@ -245,27 +281,6 @@
 
     lay(8)
     lay(32)
-    arrived(1)
-    lay(16)
-    turned(2)
-
-    @pl.when(up)
-    def _():
-        edge(1).wait_recv()
-
-    lay(0)
-    turned(0)
-    arrived(2)
-    lay(24)
-    turned(1)
-
-    @pl.when(down)
-    def _():
-        edge(-1).wait_recv()
-
-    lay(40)
-    turned(3)
-
     def part(e, way):
         dr, dc = WAYS[way]
         at, size, to = {0: (8, ROWS, 8), -1: (8, 8, 40), 1: (32, 8, 0)}[dr]
@@ -292,11 +307,38 @@
             def _(way=way):
                 part(e, way).wait_recv()
 
-    total = lax.fori_loop(
-        0, FRAMES, lambda p, t: t + recv[p, 8:40, :], jnp.zeros((ROWS, LANES), jnp.float32)
-    )
-    est[0, 1, 8:40, :] = total / FRAMES
+    def start(at):
+        total = lax.fori_loop(
+            0, FRAMES, lambda p, t: t + recv[p, at : at + 8, :], jnp.zeros((8, LANES), jnp.float32),
+            unroll=16,
+        )
+        est[0, 1, at : at + 8, :] = total / FRAMES
+
+    start(8)
+    start(32)
+    arrived(1)
+    start(16)
+    lay(16)
+    turned(2)
+
+    @pl.when(up)
+    def _():
+        edge(1).wait_recv()
+
+    lay(0)
+    turned(0)
+    arrived(2)
+    start(24)
     give(0)
+    lay(24)
+    turned(1)
+
+    @pl.when(down)
+    def _():
+        edge(-1).wait_recv()
+
+    lay(40)
+    turned(3)
 
     for dc in (-1, 1):
 
@@ -311,7 +353,7 @@
         for i, s in enumerate(windows([tf[i, at, :] for i in range(32)], 24)):
             rowbox[i, at, :] = s
 
-    @pl.loop(0, 24)
+    @pl.loop(0, 24, unroll=4)
     def _(i):
         mean[i] = down_sum(rowbox[i]) * area[i]
 
@@ -328,22 +370,28 @@
 
         mean_guide = smooth(guide)
         variance = smooth(guide * guide) - mean_guide * mean_guide
-        keep(guide, mean_guide, inside / (variance + GUIDE_EPS))
-
-        @pl.loop(0, 18)
+        guide_t[...] = stacked(guide)
+        stat_t[...] = stacked(mean_guide, inside / (variance + GUIDE_EPS))
+
+        @pl.loop(0, 16, unroll=16)
+        def _(q):
+            two = jnp.dot(guide_t[...], pick_g[q], preferred_element_type=jnp.float32)
+            gb[2 * q] = two[:, 0:LANES]
+            gb[2 * q + 1] = two[:, LANES:]
+
+        @pl.loop(0, 18, unroll=2)
         def _(j):
             at = pl.ds(pl.multiple_of(j * 8, 8), 8)
-            t = table[at, :]
-            products = [tf[i, at, :] * spread(t, i) for i in range(32)]
+            products = [tf[i, at, :] * gb[i, at, :] for i in range(32)]
             for i, s in enumerate(windows(products, 24)):
                 rowbox[i, at, :] = s
 
-        @pl.loop(0, 24)
+        @pl.loop(0, 24, unroll=8)
         def _(i):
-            t = table[0:136, :]
-            guided = spread(t, 48 + i)
+            both = jnp.dot(stat_t[...], pick_s[i], preferred_element_type=jnp.float32)
+            guided = both[0:136, 0:LANES]
             m = mean[i]
-            sl = (down_sum(rowbox[i]) * area[i] - guided * m) * spread(t, 88 + i)
+            sl = (down_sum(rowbox[i]) * area[i] - guided * m) * both[0:136, LANES:]
             slope[i] = sl
             offset[i] = m - sl * guided
 
@@ -355,21 +403,22 @@
                     dst[i, at, :] = s
 
         wide = lax.broadcasted_iota(jnp.int32, (LANES, LANES), 1)
-        low = wide < HALF
+        late = wide % HALF >= 32
 
         def weigh(i, acc):
-            center = spread(table[8:136, :], 8 + i)
+            center = gb[8 + i, 8:136, :]
             filtered = (down_sum(box1[i]) * center + down_sum(box2[i])) * area[i + 4, 4:132, :]
             gap = (filtered - center) * (1.0 / CAUCHY_SCALE)
-            weight = 1.0 / (1.0 + gap * gap)
-            for x, at in ((weight, 0), (weight * tf[i + 8, 8:136, :], 16)):
-                a = jnp.sum(jnp.where(low, x, 0.0), axis=1, keepdims=True)
-                b = jnp.sum(jnp.where(low, 0.0, x), axis=1, keepdims=True)
-                acc = jnp.where(wide == at + i, a, acc)
-                acc = jnp.where(wide == HALF + at + i, b, acc)
-            return acc
-
-        acc = lax.fori_loop(0, PAIR, weigh, jnp.zeros((LANES, LANES), jnp.float32)).T
+            w = 1.0 / (1.0 + gap * gap)
+            wp = w * tf[i + 8, 8:136, :]
+            part_sums = jnp.where(late, w + pltpu.roll(w, 32, 1), wp + pltpu.roll(wp, 96, 1))
+            return acc + jnp.dot(
+                jnp.concatenate(thirds(part_sums), axis=1),
+                pick_w[i],
+                preferred_element_type=jnp.float32,
+            )
+
+        acc = lax.fori_loop(0, PAIR, weigh, jnp.zeros((LANES, LANES), jnp.float32), unroll=8).T
         new = jnp.concatenate(
             [acc[16:32] / acc[0:16], acc[80:96] / acc[64:80]], axis=0
         )
@@ -453,6 +502,12 @@
             pltpu.VMEM((16, 136, LANES), f32),
             pltpu.VMEM((16, 136, LANES), f32),
             pltpu.VMEM((144, LANES), f32),
+            pltpu.VMEM((32, 144, LANES), f32),
+            pltpu.VMEM((144, 256), jnp.bfloat16),
+            pltpu.VMEM((144, 256), jnp.bfloat16),
+            pltpu.VMEM((16, 256, 256), jnp.bfloat16),
+            pltpu.VMEM((24, 256, 256), jnp.bfloat16),
+            pltpu.VMEM((16, 384, LANES), jnp.bfloat16),
             pltpu.VMEM((ROUNDS, 3, WIN, LANES), f32),
             pltpu.VMEM((ROWS, LANES), f32),
             dma,

time: 93.8 us -> 75.9 us (0.81)
  Pallas kernels: 92 us -> 74.2 us
    pallas_call x1, Pallas kernels: 92 us -> 74.2 us  [merge(): pl.pallas_call(functools.partial(kernel, nf, nr), out_shape=jax.ShapeDtyp...]
where the time goes in v2:
time: 75.9 us; the launch traced here: 75.8 us
  Pallas kernels  74.2 us (98%)
  local copies, waits for them, and re-layouts  1.67 us (2%)
    pallas_call x1, Pallas kernels, merge(): pl.pallas_call(functools.partial(kernel, nf, nr), out_shape=jax.ShapeDtyp...  74.2 us
    unnamed x1, local copies, waits for them, and re-layouts  1.67 us

profile of v2, /device:TPU:4, one launch (start us, length us, event | category | flops | bytes accessed | tf_op | source)
XLA Modules:
  0.0 75.8 jit_solution(612617547295456980)
XLA Ops:
  0.0 74.2 %merge.1 = f32[32,2048]{1,0:T(8,128)} custom-call(f32[4,32,2048]{2,1,0:T(8,128)} %frames.1), custom_call_target="tpu_custom_call" | custom-call | tf_op jit(solution)/shard_map/merge/pallas_call | solution.py:488
  74.2 1.7 %copy.3 = f32[32,2048]{1,0:T(8,128)} copy(f32[32,2048]{1,0:T(8,128)} %merge.1) | data formatting | bytes 524288

commit v3 on v2

--- a/solution.py
+++ b/solution.py
@@ -72,8 +72,8 @@
 
 
 def kernel(
-    nf, nr, frames, out, recv, flat, tf, rowbox, mean, area, slope, offset, box1, box2,
-    table, gb, guide_t, stat_t, pick_g, pick_s, pick_w, est, fin, own_sem, a2a_send, a2a_recv, row_send, row_recv, col_send,
+    nf, nr, frames, out, recv, flat, tf, rowbox, rowmean, mean, area, slope, offset, box1, box2,
+    table, gb, guide_t, stat_t, pick_g, pick_s, pick_w, est, fin, turned_sums, own_sem, a2a_send, a2a_recv, row_send, row_recv, col_send,
     col_recv, est_send, est_recv, fin_send, fin_recv,
 ):
     per = FRAMES // nf
@@ -82,6 +82,8 @@
     c = snake(f)
     up, down = r > 0, r < nr - 1
     left, right = c > 0, c < nf - 1
+    odd = r % 2 == 1
+    first = 8 * (r % 2)
     left_f = snake(jnp.maximum(c - 1, 0))
     right_f = snake(jnp.minimum(c + 1, nf - 1))
 
@@ -293,12 +295,21 @@
             device_id_type=MESH,
         )
 
-    def give(e):
-        for way, (dr, dc) in enumerate(WAYS):
-
-            @pl.when(there(dr, dc))
+    def give(e, ways):
+        for way in ways:
+
+            @pl.when(there(*WAYS[way]))
             def _(way=way):
                 part(e, way).start()
+
+    def give_rows(e, late):
+        @pl.when(odd != late)
+        def _():
+            give(e, (3, 6, 7))
+
+        @pl.when(odd == late)
+        def _():
+            give(e, (2, 4, 5))
 
     def take(e):
         for way, (dr, dc) in enumerate(WAYS):
@@ -316,6 +327,8 @@
 
     start(8)
     start(32)
+    give_rows(0, False)
+    give_rows(0, True)
     arrived(1)
     start(16)
     lay(16)
@@ -329,7 +342,7 @@
     turned(0)
     arrived(2)
     start(24)
-    give(0)
+    give(0, (0, 1))
     lay(24)
     turned(1)
 
@@ -340,22 +353,29 @@
     lay(40)
     turned(3)
 
-    for dc in (-1, 1):
-
-        @pl.when(there(0, -dc))
-        def _(dc=dc):
-            for q in range(4):
-                side(q, dc).wait_recv()
-
-    @pl.loop(0, 18)
-    def _(j):
-        at = pl.ds(pl.multiple_of(j * 8, 8), 8)
-        for i, s in enumerate(windows([tf[i, at, :] for i in range(32)], 24)):
-            rowbox[i, at, :] = s
-
-    @pl.loop(0, 24, unroll=4)
-    def _(i):
-        mean[i] = down_sum(rowbox[i]) * area[i]
+    def tile(j):
+        return pl.ds(pl.multiple_of(j * 8, 8), 8)
+
+    def own_rows(j):
+        for i, s in enumerate(windows([tf[i, tile(j), :] for i in range(32)], 24)):
+            rowmean[i, tile(j), :] = s
+
+    def guided_rows(j):
+        for i, s in enumerate(windows([tf[i, tile(j), :] * gb[i, tile(j), :] for i in range(32)], 24)):
+            rowbox[i, tile(j), :] = s
+
+    pl.loop(1, 17, unroll=2)(own_rows)
+
+    def final(late, of, to):
+        rows = pl.ds(pl.multiple_of(8 - first if late else first, 8), 8)
+        return pltpu.make_async_remote_copy(
+            src_ref=fin.at[:, rows, :],
+            dst_ref=out.at[:, rows, pl.ds(pl.multiple_of(snake(of) * LANES, LANES), LANES)],
+            send_sem=fin_send.at[late, to],
+            recv_sem=fin_recv.at[late, of],
+            device_id={"frame": to, "row": r},
+            device_id_type=MESH,
+        )
 
     for e in range(ROUNDS):
         take(e)
@@ -379,14 +399,27 @@
             gb[2 * q] = two[:, 0:LANES]
             gb[2 * q + 1] = two[:, LANES:]
 
-        @pl.loop(0, 18, unroll=2)
-        def _(j):
-            at = pl.ds(pl.multiple_of(j * 8, 8), 8)
-            products = [tf[i, at, :] * gb[i, at, :] for i in range(32)]
-            for i, s in enumerate(windows(products, 24)):
-                rowbox[i, at, :] = s
-
-        @pl.loop(0, 24, unroll=8)
+        pl.loop(1, 17, unroll=4)(guided_rows)
+
+        if e == 0:
+            for dc in (-1, 1):
+
+                @pl.when(there(0, -dc))
+                def _(dc=dc):
+                    for q in range(4):
+                        side(q, dc).wait_recv()
+
+            own_rows(0)
+            own_rows(17)
+
+            @pl.loop(0, 24, unroll=4)
+            def _(i):
+                mean[i] = down_sum(rowmean[i]) * area[i]
+
+        guided_rows(0)
+        guided_rows(17)
+
+        @pl.loop(0, 24, unroll=12)
         def _(i):
             both = jnp.dot(stat_t[...], pick_s[i], preferred_element_type=jnp.float32)
             guided = both[0:136, 0:LANES]
@@ -395,7 +428,7 @@
             slope[i] = sl
             offset[i] = m - sl * guided
 
-        @pl.loop(0, 17)
+        @pl.loop(0, 17, unroll=17)
         def _(j):
             at = pl.ds(pl.multiple_of(j * 8, 8), 8)
             for src, dst in ((slope, box1), (offset, box2)):
@@ -403,7 +436,7 @@
                     dst[i, at, :] = s
 
         wide = lax.broadcasted_iota(jnp.int32, (LANES, LANES), 1)
-        late = wide % HALF >= 32
+        upper = wide % HALF >= 32
 
         def weigh(i, acc):
             center = gb[8 + i, 8:136, :]
@@ -411,39 +444,41 @@
             gap = (filtered - center) * (1.0 / CAUCHY_SCALE)
             w = 1.0 / (1.0 + gap * gap)
             wp = w * tf[i + 8, 8:136, :]
-            part_sums = jnp.where(late, w + pltpu.roll(w, 32, 1), wp + pltpu.roll(wp, 96, 1))
+            part_sums = jnp.where(upper, w + pltpu.roll(w, 32, 1), wp + pltpu.roll(wp, 96, 1))
             return acc + jnp.dot(
                 jnp.concatenate(thirds(part_sums), axis=1),
                 pick_w[i],
                 preferred_element_type=jnp.float32,
             )
 
-        acc = lax.fori_loop(0, PAIR, weigh, jnp.zeros((LANES, LANES), jnp.float32), unroll=8).T
-        new = jnp.concatenate(
-            [acc[16:32] / acc[0:16], acc[80:96] / acc[64:80]], axis=0
-        )
-        if e < ROUNDS - 1:
-            est[e + 1, 1, 8:40, :] = new
-            give(e + 1)
-        else:
-            fin[...] = new
-
-    def final(of, to):
-        return pltpu.make_async_remote_copy(
-            src_ref=fin,
-            dst_ref=out.at[:, pl.ds(pl.multiple_of(snake(of) * LANES, LANES), LANES)],
-            send_sem=fin_send.at[to],
-            recv_sem=fin_recv.at[of],
-            device_id={"frame": to, "row": r},
-            device_id_type=MESH,
-        )
-
-    @pl.loop(1, nf)
-    def _(s):
-        final(f, (f + step_of(s)) % nf).start()
+        for late, at in enumerate((first, 8 - first)):
+            at = pl.multiple_of(at, 8)
+            turned_sums[...] = lax.fori_loop(
+                0,
+                8,
+                lambda i, acc: weigh(at + i, acc),
+                jnp.zeros((LANES, LANES), jnp.float32),
+                unroll=8,
+            ).T
+            for half in range(2):
+                total = turned_sums[pl.ds(half * HALF + at, 8), :]
+                new = turned_sums[pl.ds(half * HALF + 16 + at, 8), :] / total
+                if e < ROUNDS - 1:
+                    est[e + 1, 1, pl.ds(8 + half * PAIR + at, 8), :] = new
+                else:
+                    fin[half, pl.ds(at, 8), :] = new
+            if e < ROUNDS - 1:
+                give_rows(e + 1, bool(late))
+                if late:
+                    give(e + 1, (0, 1))
+            else:
+
+                @pl.loop(1, nf)
+                def _(s, late=late):
+                    final(late, f, (f + step_of(s)) % nf).start()
 
     mine = pltpu.make_async_copy(
-        fin, out.at[:, pl.ds(pl.multiple_of(c * LANES, LANES), LANES)], own_sem
+        fin, out.at[:, :, pl.ds(pl.multiple_of(c * LANES, LANES), LANES)], own_sem
     )
     mine.start()
 
@@ -476,8 +511,9 @@
     @pl.loop(1, nf)
     def _(s):
         peer = (f + s) % nf
-        final(peer, peer).wait_recv()
-        final(f, peer).wait_send()
+        for late in range(2):
+            final(late, peer, peer).wait_recv()
+            final(late, f, peer).wait_send()
 
     mine.wait()
 
@@ -487,13 +523,14 @@
     dma = pltpu.SemaphoreType.DMA
     return pl.pallas_call(
         functools.partial(kernel, nf, nr),
-        out_shape=jax.ShapeDtypeStruct((ROWS, nf * LANES), f32),
+        out_shape=jax.ShapeDtypeStruct((2, PAIR, nf * LANES), f32),
         in_specs=[pl.BlockSpec(memory_space=pl.ANY)],
         out_specs=pl.BlockSpec(memory_space=pl.ANY),
         scratch_shapes=[
             pltpu.VMEM((FRAMES, WIN, LANES), f32),
             pltpu.VMEM((FRAMES * PITCH, LANES), f32),
             pltpu.VMEM((32, 144, LANES), f32),
+            pltpu.VMEM((24, 144, LANES), f32),
             pltpu.VMEM((24, 144, LANES), f32),
             pltpu.VMEM((24, 136, LANES), f32),
             pltpu.VMEM((24, 136, LANES), f32),
@@ -509,7 +546,8 @@
             pltpu.VMEM((24, 256, 256), jnp.bfloat16),
             pltpu.VMEM((16, 384, LANES), jnp.bfloat16),
             pltpu.VMEM((ROUNDS, 3, WIN, LANES), f32),
-            pltpu.VMEM((ROWS, LANES), f32),
+            pltpu.VMEM((2, PAIR, LANES), f32),
+            pltpu.VMEM((LANES, LANES), f32),
             dma,
             dma((4, nf)),
             dma((4, nf)),
@@ -519,12 +557,12 @@
             dma((2, 4)),
             dma((ROUNDS, 8)),
             dma((ROUNDS, 8)),
-            dma((nf,)),
-            dma((nf,)),
+            dma((2, nf)),
+            dma((2, nf)),
         ],
         compiler_params=pltpu.CompilerParams(collective_id=0, has_side_effects=True),
         name="merge",
-    )(frames)
+    )(frames).reshape(ROWS, nf * LANES)
 
 
 def solution(mesh):

time: 75.9 us -> 72.6 us (0.957)
  Pallas kernels: 74.2 us -> 70.8 us
    pallas_call x1, Pallas kernels: 74.2 us -> 70.8 us  [merge(): pl.pallas_call(functools.partial(kernel, nf, nr), out_shape=jax.ShapeDtyp...]
where the time goes in v3:
time: 72.6 us; the launch traced here: 72.5 us
  Pallas kernels  70.8 us (98%)
  local copies, waits for them, and re-layouts  1.67 us (2%)
    pallas_call x1, Pallas kernels, merge(): pl.pallas_call(functools.partial(kernel, nf, nr), out_shape=jax.ShapeDtyp...  70.8 us
    unnamed x1, local copies, waits for them, and re-layouts  1.67 us

profile of v3, /device:TPU:4, one launch (start us, length us, event | category | flops | bytes accessed | tf_op | source)
XLA Modules:
  0.0 72.5 jit_solution(8522356252131413788)
XLA Ops:
  0.0 70.8 %merge.1 = f32[2,16,2048]{2,1,0:T(8,128)} custom-call(f32[4,32,2048]{2,1,0:T(8,128)} %frames.1), custom_call_target="tpu_custom_call" | custom-call | tf_op jit(solution)/shard_map/merge/pallas_call | solution.py:524
  70.8 1.7 %copy.3 = f32[32,2048]{1,0:T(8,128)} copy(f32[32,2048]{1,0:T(8,128)} %bitcast.1) | data formatting | bytes 524288

commit v4 on v3

--- a/solution.py
+++ b/solution.py
@@ -107,30 +107,36 @@
     )
     own.start()
 
-    est[...] = jnp.zeros_like(est)
-
     @pl.when(jnp.logical_not(up))
     def _():
         recv[:, 0:8, :] = jnp.zeros((FRAMES, 8, LANES), jnp.float32)
+        est[:, :, 0:8, :] = jnp.zeros((ROUNDS, 3, 8, LANES), jnp.float32)
 
     @pl.when(jnp.logical_not(down))
     def _():
         recv[:, 40:48, :] = jnp.zeros((FRAMES, 8, LANES), jnp.float32)
+        est[:, :, 40:48, :] = jnp.zeros((ROUNDS, 3, 8, LANES), jnp.float32)
 
     @pl.when(jnp.logical_not(left))
     def _():
         tf[:, 0:8, :] = jnp.zeros((32, 8, LANES), jnp.float32)
+        est[:, 0] = jnp.zeros((ROUNDS, WIN, LANES), jnp.float32)
 
     @pl.when(jnp.logical_not(right))
     def _():
         tf[:, 136:144, :] = jnp.zeros((32, 8, LANES), jnp.float32)
+        est[:, 2] = jnp.zeros((ROUNDS, WIN, LANES), jnp.float32)
+
+    def step_of(s):
+        d = (s + 1) // 2
+        return jnp.where(s % 2 == 1, d, nf - d)
 
     barrier = pltpu.get_barrier_semaphore()
 
     @pl.loop(1, nf)
     def _(s):
         pl.semaphore_signal(
-            barrier, inc=1, device_id={"frame": (f + s) % nf, "row": r}, device_id_type=MESH
+            barrier, inc=1, device_id={"frame": (f + step_of(nf - s)) % nf, "row": r}, device_id_type=MESH
         )
 
     others = jnp.int32(nf - 1)
@@ -157,16 +163,12 @@
             device_id_type=MESH,
         )
 
-    def step_of(s):
-        d = (s + 1) // 2
-        return jnp.where(s % 2 == 1, d, nf - d)
-
     order = (0, 3, 1, 2)
     for k in order:
 
         @pl.loop(1, nf)
         def _(s, k=k):
-            block(k, f, (f + step_of(s)) % nf).start()
+            block(k, f, (f + step_of(nf - s)) % nf).start()
 
     def arrived(k):
         @pl.loop(1, nf)
@@ -340,17 +342,17 @@
 
     lay(0)
     turned(0)
+    @pl.when(down)
+    def _():
+        edge(-1).wait_recv()
+
+    lay(40)
     arrived(2)
     start(24)
     give(0, (0, 1))
     lay(24)
     turned(1)
 
-    @pl.when(down)
-    def _():
-        edge(-1).wait_recv()
-
-    lay(40)
     turned(3)
 
     def tile(j):
@@ -419,7 +421,7 @@
         guided_rows(0)
         guided_rows(17)
 
-        @pl.loop(0, 24, unroll=12)
+        @pl.loop(0, 24, unroll=24)
         def _(i):
             both = jnp.dot(stat_t[...], pick_s[i], preferred_element_type=jnp.float32)
             guided = both[0:136, 0:LANES]
@@ -475,7 +477,7 @@
 
                 @pl.loop(1, nf)
                 def _(s, late=late):
-                    final(late, f, (f + step_of(s)) % nf).start()
+                    final(late, f, (f + step_of(nf - s)) % nf).start()
 
     mine = pltpu.make_async_copy(
         fin, out.at[:, :, pl.ds(pl.multiple_of(c * LANES, LANES), LANES)], own_sem

time: 72.6 us -> 70.6 us (0.972)
  Pallas kernels: 70.8 us -> 68.4 us
    pallas_call x1, Pallas kernels: 70.8 us -> 68.4 us  [merge(): pl.pallas_call(functools.partial(kernel, nf, nr), out_shape=jax.ShapeDtyp...]
where the time goes in v4:
time: 70.6 us; the launch traced here: 70.1 us
  Pallas kernels  68.4 us (97%)
  local copies, waits for them, and re-layouts  1.67 us (2%)
    pallas_call x1, Pallas kernels, merge(): pl.pallas_call(functools.partial(kernel, nf, nr), out_shape=jax.ShapeDtyp...  68.4 us
    unnamed x1, local copies, waits for them, and re-layouts  1.67 us

profile of v4, /device:TPU:4, one launch (start us, length us, event | category | flops | bytes accessed | tf_op | source)
XLA Modules:
  0.0 70.1 jit_solution(14811454169030651522)
XLA Ops:
  0.0 68.4 %merge.1 = f32[2,16,2048]{2,1,0:T(8,128)} custom-call(f32[4,32,2048]{2,1,0:T(8,128)} %frames.1), custom_call_target="tpu_custom_call" | custom-call | tf_op jit(solution)/shard_map/merge/pallas_call | solution.py:526
  68.4 1.7 %copy.3 = f32[32,2048]{1,0:T(8,128)} copy(f32[32,2048]{1,0:T(8,128)} %bitcast.1) | data formatting | bytes 524288

commit v5 on v4

--- a/solution.py
+++ b/solution.py
@@ -307,11 +307,11 @@
     def give_rows(e, late):
         @pl.when(odd != late)
         def _():
-            give(e, (3, 6, 7))
+            give(e, (6, 7, 3))
 
         @pl.when(odd == late)
         def _():
-            give(e, (2, 4, 5))
+            give(e, (4, 5, 2))
 
     def take(e):
         for way, (dr, dc) in enumerate(WAYS):
@@ -366,7 +366,7 @@
         for i, s in enumerate(windows([tf[i, tile(j), :] * gb[i, tile(j), :] for i in range(32)], 24)):
             rowbox[i, tile(j), :] = s
 
-    pl.loop(1, 17, unroll=2)(own_rows)
+    pl.loop(1, 17, unroll=4)(own_rows)
 
     def final(late, of, to):
         rows = pl.ds(pl.multiple_of(8 - first if late else first, 8), 8)
@@ -401,7 +401,7 @@
             gb[2 * q] = two[:, 0:LANES]
             gb[2 * q + 1] = two[:, LANES:]
 
-        pl.loop(1, 17, unroll=4)(guided_rows)
+        pl.loop(1, 17, unroll=8)(guided_rows)
 
         if e == 0:
             for dc in (-1, 1):
@@ -414,7 +414,7 @@
             own_rows(0)
             own_rows(17)
 
-            @pl.loop(0, 24, unroll=4)
+            @pl.loop(0, 24, unroll=12)
             def _(i):
                 mean[i] = down_sum(rowmean[i]) * area[i]
 

time: 70.6 us -> 70.5 us (level)
  no operation moved by 1% of the time
where the time goes in v5:
time: 70.5 us; the launch traced here: 70 us
  Pallas kernels  68.4 us (97%)
  local copies, waits for them, and re-layouts  1.67 us (2%)
    pallas_call x1, Pallas kernels, merge(): pl.pallas_call(functools.partial(kernel, nf, nr), out_shape=jax.ShapeDtyp...  68.4 us
    unnamed x1, local copies, waits for them, and re-layouts  1.67 us

profile of v5, /device:TPU:4, one launch (start us, length us, event | category | flops | bytes accessed | tf_op | source)
XLA Modules:
  0.0 70.0 jit_solution(2957089899469128902)
XLA Ops:
  0.0 68.4 %merge.1 = f32[2,16,2048]{2,1,0:T(8,128)} custom-call(f32[4,32,2048]{2,1,0:T(8,128)} %frames.1), custom_call_target="tpu_custom_call" | custom-call | tf_op jit(solution)/shard_map/merge/pallas_call | solution.py:526
  68.4 1.7 %copy.3 = f32[32,2048]{1,0:T(8,128)} copy(f32[32,2048]{1,0:T(8,128)} %bitcast.1) | data formatting | bytes 524288
